TPU v7x, 32 devices: a whole 2x2x4 slice. The times are simulated.
32 devices in a mesh: frame: 8 (over z, x), row: 4 (over y, core).
Axes of the slice: x: 2, y: 2, z: 4, core: 2. Of those that a mesh axis runs over, the one named last changes fastest.
Arguments:
- clip: bfloat16 [16, 16, 256, 128], P('frame', 'row'), may hold values from -6 to 6
- first_kernel: bfloat16 [3, 3, 3, 128, 128], replicated, may hold values from -0.109375 to 0.109375
- second_kernel: bfloat16 [3, 3, 3, 128, 128], replicated, may hold values from -0.109375 to 0.109375
- cotangent: bfloat16 [16, 16, 256, 128], P('frame', 'row'), may hold values from -6 to 6
Outputs:
- critic_map: bfloat16 [16, 16, 256, 128], P('frame', 'row')
- clip_grad: bfloat16 [16, 16, 256, 128], P('frame', 'row')
- first_grad: float32 [3, 3, 3, 128, 128], replicated
- second_grad: float32 [3, 3, 3, 128, 128], replicated
All inputs are finite; a program needn't handle non-finite values.
Results may differ from a plain program's by a relative error of at most 0.012.
Values may be sent and summed in bfloat16 or wider, within the bound.
A program may use at most 64 MiB of HBM per device.

v0:
```python
import functools

import jax
import jax.numpy as jnp
from jax import lax
from jax.experimental import pallas as pl
from jax.experimental.pallas import tpu as pltpu
from jax.sharding import PartitionSpec as P

MESH = pl.DeviceIdType.MESH
BF16, F32 = jnp.bfloat16, jnp.float32


def silu_slope(value):
    sigma = jax.nn.sigmoid(value)
    return sigma * (1.0 + value * (1.0 - sigma))


def kernel(
    n_frame, n_row, grad_scale,
    clip, w1, w2, cot,
    critic, clip_grad, g1, g2,
    pads, cols0, cols1, cols2, cols3, w1t, w2t, acc, slope1,
    f_send, f_recv, r_send, r_recv,
):
    cols = (cols0, cols1, cols2, cols3)
    _, rows, width, ch = clip.shape
    me_f, me_r = lax.axis_index("frame"), lax.axis_index("row")
    later, earlier = me_f < n_frame - 1, me_f > 0
    below, above = me_r < n_row - 1, me_r > 0
    sides = (
        (later, {"frame": me_f + 1}), (earlier, {"frame": me_f - 1}),
        (below, {"row": me_r + 1}), (above, {"row": me_r - 1}),
    )
    barrier = pltpu.get_barrier_semaphore()
    for there, who in sides:
        @pl.when(there)
        def _():
            pl.semaphore_signal(barrier, inc=1, device_id=who, device_id_type=MESH)

    def zero(ref):
        ref[...] = jnp.zeros(ref.shape, ref.dtype)

    for k in range(4):
        fwd = k < 2

        @pl.when(jnp.logical_not(earlier if fwd else later))
        def _():
            for f in ((0, 1) if fwd else (2, 3)):
                zero(pads.at[k, f])
        local = (2, 3) if fwd else (0, 1)
        halo = (0, 1) if fwd else (2, 3)
        for f in range(4):
            @pl.when(jnp.logical_not(above))
            def _():
                zero(pads.at[k, f, 0])

            @pl.when(jnp.logical_not(below))
            def _():
                zero(pads.at[k, f, rows + 1])
    for t in range(2):
        pads[0, 2 + t, 1 : rows + 1] = clip[t]
    peers = sum(there.astype(jnp.int32) for there, _ in sides)
    pl.semaphore_wait(barrier, peers)

    def frame_copy(k, t):
        fwd = k < 2
        base, hbase = (2, 0) if fwd else (0, 2)
        return pltpu.make_async_remote_copy(
            src_ref=pads.at[k, base + t, pl.ds(1, rows)],
            dst_ref=pads.at[k, hbase + t, pl.ds(1, rows)],
            send_sem=f_send.at[k, t],
            recv_sem=f_recv.at[k, t],
            device_id={"frame": me_f + 1 if fwd else me_f - 1},
            device_id_type=MESH,
        )

    def row_copy(k, f, way):
        src, dst = ((rows, 0), (1, rows + 1))[way]
        return pltpu.make_async_remote_copy(
            src_ref=pads.at[k, f, src],
            dst_ref=pads.at[k, f, dst],
            send_sem=r_send.at[k, f, way],
            recv_sem=r_recv.at[k, f, way],
            device_id={"row": me_r + 1 if way == 0 else me_r - 1},
            device_id_type=MESH,
        )

    def send_rows(k, f):
        @pl.when(below)
        def _():
            row_copy(k, f, 0).start()

        @pl.when(above)
        def _():
            row_copy(k, f, 1).start()

    def wait_rows(k, f):
        @pl.when(above)
        def _():
            row_copy(k, f, 0).wait_recv()

        @pl.when(below)
        def _():
            row_copy(k, f, 1).wait_recv()

    def publish(k, t):
        @pl.when(later if k < 2 else earlier)
        def _():
            frame_copy(k, t).start()
        send_rows(k, (2 if k < 2 else 0) + t)

    def build(k, f):
        def one(r, c):
            x = pads[k, f, r].astype(F32)
            pos = lax.broadcasted_iota(jnp.int32, (width, ch), 0)
            left = jnp.where(pos == 0, 0.0, pltpu.roll(x, 1, 0))
            right = jnp.where(pos == width - 1, 0.0, pltpu.roll(x, width - 1, 0))
            cols[k][f, r, :, 0:ch] = left.astype(BF16)
            cols[k][f, r, :, ch : 2 * ch] = pads[k, f, r]
            cols[k][f, r, :, 2 * ch : 3 * ch] = right.astype(BF16)
            return c
        lax.fori_loop(0, rows + 2, one, 0)

    STEP = 2

    def taps(k, w, t, frames, h, z):
        for a in range(3):
            if t + a not in frames:
                continue
            for b in range(3):
                x = cols[k][t + a, pl.ds(h * STEP + b, STEP)].reshape(STEP * width, 3 * ch)
                d = jnp.dot(x, w[a, b], preferred_element_type=F32)
                z = d if z is None else z + d
        return z

    def stage(k, w, epilogue, between):
        fwd = k < 2
        order = (1, 0) if fwd else (0, 1)
        local, halo = ((2, 3), (0, 1)) if fwd else ((0, 1), (2, 3))
        for t in order:
            wait_rows(k, local[t])
            build(k, local[t])
        for t in order:
            def part(h, c):
                z = taps(k, w, t, local, h, None)
                acc[t, pl.ds(h * STEP, STEP)] = z.reshape(STEP, width, ch)
                return c
            lax.fori_loop(0, rows // STEP, part, 0)
        between()
        for t in order:
            @pl.when(earlier if fwd else later)
            def _():
                frame_copy(k, t).wait_recv()
                send_rows(k, halo[t])
                wait_rows(k, halo[t])
            build(k, halo[t])

            def rest(h, c):
                z = taps(k, w, t, halo, h, acc[t, pl.ds(h * STEP, STEP)].reshape(STEP * width, ch))
                epilogue(t, pl.ds(h * STEP, STEP), h * STEP, z.reshape(STEP, width, ch))
                return c
            lax.fori_loop(0, rows // STEP, rest, 0)
            if k < 3:
                publish(k + 1, t)

    for t in (1, 0):
        publish(0, t)

    def turn_weights():
        def one(i, c):
            a, b = i // 3, lax.rem(i, 3)
            for src, dst in ((w1, w1t), (w2, w2t)):
                for q in range(3):
                    block = src[2 - a, 2 - b, pl.ds((2 - q) * ch, ch), :]
                    dst[a, b, pl.ds(q * ch, ch), :] = block.astype(F32).T.astype(BF16)
            return c
        lax.fori_loop(0, 9, one, 0)

    def weight_grad(kx, kd, out):
        def one(i, c):
            a, b = i // 3, lax.rem(i, 3)
            total = None
            for t in range(2):
                x = cols[kx][t + a, pl.ds(b, rows)].reshape(rows * width, 3 * ch)
                d = pads[kd, t, 1 : rows + 1].reshape(rows * width, ch)
                p = lax.dot_general(x, d, (((0,), (0,)), ((), ())), preferred_element_type=F32)
                total = p if total is None else total + p
            out[a, b] = (total * grad_scale).astype(out.dtype)
            return c
        lax.fori_loop(0, 9, one, 0)

    def end0(t, hs, h, z):
        sigma = jax.nn.sigmoid(z)
        slope1[t, hs] = sigma * (1.0 + z * (1.0 - sigma))
        pads[1, 2 + t, pl.ds(h + 1, STEP)] = (z * sigma).astype(BF16)

    def end1(t, hs, h, z):
        sigma = jax.nn.sigmoid(z)
        critic[t, hs] = (z * sigma).astype(BF16)
        delta = cot[t, hs].astype(F32) * (sigma * (1.0 + z * (1.0 - sigma)))
        pads[2, t, pl.ds(h + 1, STEP)] = delta.astype(BF16)

    def end2(t, hs, h, z):
        pads[3, t, pl.ds(h + 1, STEP)] = (z * slope1[t, hs]).astype(BF16)

    def end3(t, hs, h, z):
        clip_grad[t, hs] = z.astype(BF16)

    stage(0, w1, end0, turn_weights)
    stage(1, w2, end1, lambda: None)
    stage(2, w2t, end2, lambda: weight_grad(1, 2, g2))
    stage(3, w1t, end3, lambda: weight_grad(0, 3, g1))

    for k in range(4):
        fwd = k < 2
        for t in range(2):
            @pl.when(later if fwd else earlier)
            def _():
                frame_copy(k, t).wait_send()
        for f in range(4):
            is_halo = (f < 2) if fwd else (f >= 2)
            has = (earlier if fwd else later) if is_halo else jnp.bool_(True)
            for way, there in ((0, below), (1, above)):
                @pl.when(jnp.logical_and(there, has) if is_halo else there)
                def _():
                    row_copy(k, f, way).wait_send()


def sum_kernel(levels, n, mine, total, buf, landing, s1, q1, s2, q2):
    peers = []
    for axis, step in levels:
        me = lax.axis_index(axis)
        bit = lax.rem(me // step, 2)
        peers.append((bit, {axis: me + (1 - 2 * bit) * step}))
    barrier = pltpu.get_barrier_semaphore()
    for _, who in peers:
        pl.semaphore_signal(barrier, inc=1, device_id=who, device_id_type=MESH)
    pl.semaphore_wait(barrier, len(peers))
    lo, size = 0, n
    for j, (bit, who) in enumerate(peers):
        size //= 2
        keep, give = lo + bit * size, lo + (1 - bit) * size
        src = mine if j == 0 else buf
        copy = pltpu.make_async_remote_copy(
            src_ref=src.at[pl.ds(give, size)],
            dst_ref=landing.at[pl.ds(size, size)],
            send_sem=s1.at[j], recv_sem=q1.at[j],
            device_id=who, device_id_type=MESH,
        )
        copy.start()
        copy.wait()
        last = size == 1

        def add(i, c):
            z = src[keep + i].astype(F32) + landing[size + i].astype(F32)
            dst = total if last else buf
            dst[keep + i] = z.astype(BF16)
            return c
        lax.fori_loop(0, size, add, 0)
        lo = keep
    for j in range(len(peers) - 1, -1, -1):
        bit, who = peers[j]
        copy = pltpu.make_async_remote_copy(
            src_ref=total.at[pl.ds(lo, size)],
            dst_ref=total.at[pl.ds(lo, size)],
            send_sem=s2.at[j], recv_sem=q2.at[j],
            device_id=who, device_id_type=MESH,
        )
        copy.start()
        copy.wait()
        lo, size = lo - bit * size, size * 2


def summed(n_frame, n_row, flat):
    n = n_frame * n_row
    levels = [("row", 1 << b) for b in range(n_row.bit_length() - 1)]
    levels += [("frame", 1 << b) for b in range(n_frame.bit_length() - 1)]
    length, ch = flat.shape
    chunk = -(-length // (16 * n)) * 16
    mine = jnp.pad(flat, ((0, chunk * n - length), (0, 0))).reshape(n, chunk, ch)
    vmem = pl.BlockSpec(memory_space=pltpu.VMEM)
    sems = pltpu.SemaphoreType.DMA((len(levels),))
    out = pl.pallas_call(
        functools.partial(sum_kernel, levels, n),
        out_shape=jax.ShapeDtypeStruct(mine.shape, BF16),
        in_specs=[vmem],
        out_specs=vmem,
        scratch_shapes=[pltpu.VMEM(mine.shape, BF16), pltpu.VMEM(mine.shape, BF16), sems, sems, sems, sems],
        compiler_params=pltpu.CompilerParams(
            collective_id=1, has_side_effects=True, vmem_limit_bytes=32 * 2**20
        ),
    )(mine)
    return out.reshape(n * chunk, ch)[:length]


def on_device(n_frame, n_row, clip, first_kernel, second_kernel, cotangent):
    frames, rows, width, ch = clip.shape
    grad_scale = 1.0 / float(frames * n_frame * rows * n_row * width) ** 0.5
    vmem = pl.BlockSpec(memory_space=pltpu.VMEM)
    cols = pltpu.VMEM((4, rows + 2, width, 3 * ch), BF16)
    weights = (3, 3, 3 * ch, ch)
    critic, clip_grad, g1, g2 = pl.pallas_call(
        functools.partial(kernel, n_frame, n_row, grad_scale),
        out_shape=(
            jax.ShapeDtypeStruct(clip.shape, BF16),
            jax.ShapeDtypeStruct(clip.shape, BF16),
            jax.ShapeDtypeStruct(weights, BF16),
            jax.ShapeDtypeStruct(weights, BF16),
        ),
        in_specs=[vmem] * 4,
        out_specs=(vmem,) * 4,
        scratch_shapes=[
            pltpu.VMEM((4, 4, rows + 2, width, ch), BF16),
            cols, cols, cols, cols,
            pltpu.VMEM(weights, BF16),
            pltpu.VMEM(weights, BF16),
            pltpu.VMEM(clip.shape, F32),
            pltpu.VMEM(clip.shape, F32),
            pltpu.SemaphoreType.DMA((4, 2)),
            pltpu.SemaphoreType.DMA((4, 2)),
            pltpu.SemaphoreType.DMA((4, 4, 2)),
            pltpu.SemaphoreType.DMA((4, 4, 2)),
        ],
        compiler_params=pltpu.CompilerParams(
            collective_id=0, has_side_effects=True, vmem_limit_bytes=60 * 2**20
        ),
    )(clip, first_kernel.reshape(weights), second_kernel.reshape(weights), cotangent)
    shape = first_kernel.shape
    flat = jnp.concatenate([g1.reshape(-1, ch), g2.reshape(-1, ch)])
    both = summed(n_frame, n_row, flat)
    g1, g2 = both[: both.shape[0] // 2], both[both.shape[0] // 2 :]
    return critic, clip_grad, g1.astype(F32).reshape(shape), g2.astype(F32).reshape(shape)


def solution(mesh):
    placed = (P("frame", "row", None, None), P(), P(), P("frame", "row", None, None))
    return jax.shard_map(
        functools.partial(on_device, mesh.shape["frame"], mesh.shape["row"]),
        mesh=mesh,
        in_specs=placed,
        out_specs=(P("frame", "row", None, None), P("frame", "row", None, None), P(), P()),
        check_vma=False,
    )
```

profile of v0, /device:TPU:0, one launch (start us, length us, event | category | flops | bytes accessed | tf_op | source)
XLA Modules:
  0.0 142.7 jit_solution(9380060440367546247)
XLA Ops:
  0.6 74.2 %shard_map.75 = (bf16[2,4,256,128]{3,2,1,0:T(8,128)(2,1)}, bf16[2,4,256,128]{3,2,1,0:T(8,128)(2,1)}, bf16[3,3,384,128]{3,2,1,0:T(8,128)(2,1)}, bf16[3,3,384,128]{3,2,1,0:T(8,128)(2,1)}) custom-call(bf16[2,4,256,128]{3,2,1,0:T(8,128)(2,1)} %clip.1, bf16[3,3,384,128]{3,2,1,0:T(8,128)(2,1)} %bitcast.16, bf16[3,3,384,128]{3,2,1,0:T(8,128)(2,1)} %bitcast.17, ...), custom_call_target="tpu_custom_call" | custom-call | tf_op jit(solution)/shard_map/pallas_call | solution.py:303
  74.9 1.6 %fusion.2 = bf16[7168,128]{1,0:T(8,128)(2,1)S(1)} fusion(bf16[3456,128]{1,0:T(8,128)(2,1)} %bitcast.15, bf16[3456,128]{1,0:T(8,128)(2,1)} %bitcast.14), kind=kLoop, calls=%fused_computation.3 | loop fusion | flops 6422528 | bytes 3604480 | tf_op jit(solution)/shard_map/concatenate | solution.py:330
  76.4 61.7 %shard_map.76 = bf16[32,224,128]{2,1,0:T(8,128)(2,1)S(1)} custom-call(bf16[32,224,128]{2,1,0:T(8,128)(2,1)S(1)} %bitcast.10), custom_call_target="tpu_custom_call" | custom-call | tf_op jit(solution)/shard_map/pallas_call | solution.py:284
  138.2 0.1 fusion.3
  138.3 1.4 convert.2
  139.7 0.0 copy-start.1
  139.7 0.0 copy-start
  139.7 1.4 convert.3
  141.1 0.0 copy-done.1
  141.1 0.8 copy.10
  141.9 0.0 copy-done
  141.9 0.8 copy.11
Async XLA Ops:
  139.7 1.4 copy-start.1
  139.7 2.2 %copy-start = (bf16[2,4,256,128]{3,2,1,0:T(8,128)(2,1)S(1)}, bf16[2,4,256,128]{3,2,1,0:T(8,128)(2,1)}, u32[]{:S(2)}) copy-start(bf16[2,4,256,128]{3,2,1,0:T(8,128)(2,1)} %get-tuple-element.19) | copy-start | bytes 1572868
where the time goes:
time: 143 us
  Pallas kernels  136 us (95%)
  other arithmetic  4.37 us (3%)
  local copies, waits for them, and re-layouts  1.71 us (1%)
    pallas_call x1, Pallas kernels, on_device(): pl.pallas_call(functools.partial(kernel, n_frame, n_row, grad_scale), out...  74.2 us
    pallas_call x1, Pallas kernels, summed(): pl.pallas_call(functools.partial(sum_kernel, levels, n), out_shape=jax.Sh...  61.7 us

commit v1 on v0

v1 whole, which is shorter than its diff:
```python
import functools

import jax
import jax.numpy as jnp
from jax import lax
from jax.experimental import pallas as pl
from jax.experimental.pallas import tpu as pltpu
from jax.sharding import PartitionSpec as P

MESH = pl.DeviceIdType.MESH
BF16, F32 = jnp.bfloat16, jnp.float32
MARGIN = 8
HALO = 2


def sum_groups(n_frame, n_row, me_f, me_r):
    pair, member = me_f // 2, lax.rem(me_f, 2)
    side, core = me_r // 2, lax.rem(me_r, 2)
    return (
        (2, core, lambda j: {"row": side * 2 + j}),
        (n_row // 2 * 2, side * 2 + member, lambda j: {"row": j // 2 * 2 + core, "frame": pair * 2 + lax.rem(j, 2)}),
        (n_frame // 2, pair, lambda j: {"frame": j * 2 + member}),
    )


def kernel(
    n_frame, n_row, grad_scale,
    clip, w1, w2, cot,
    critic, clip_grad, total1, total2,
    pads, cross, cotp, crit_s, cg_s, slope1, w1v, w2v, w1t, w2t, xt, d3, acc,
    mine, land_a, sum_a, land_b, sum_b, land_c,
    l_sem, x_send, x_recv, o_send, o_recv, f_send, f_recv, r_send, r_recv, s_send, s_recv, t_send, t_recv,
):
    step, rows, width, ch = clip.shape
    half = width // 2
    cw = half + MARGIN
    frames = 2 * step
    me_f, me_r = lax.axis_index("frame"), lax.axis_index("row")
    member = lax.rem(me_f, 2)
    first, second = member == 0, member == 1
    later, earlier = me_f < n_frame - 2, me_f > 1
    below, above = me_r < n_row - 1, me_r > 0
    partner = {"frame": me_f + 1 - 2 * member}
    groups = sum_groups(n_frame, n_row, me_f, me_r)
    own = pl.multiple_of(member * MARGIN, MARGIN)

    def start_of(who):
        return pl.multiple_of(who * (half - MARGIN), MARGIN)

    barrier = pltpu.get_barrier_semaphore()
    for there, who in ((below, {"row": me_r + 1}), (above, {"row": me_r - 1})):
        @pl.when(there)
        def _():
            pl.semaphore_signal(barrier, inc=1, device_id=who, device_id_type=MESH)
    greeted = below.astype(jnp.int32) + above.astype(jnp.int32)
    for count, index, device in groups[1:]:
        for d in range(1, count):
            pl.semaphore_signal(barrier, inc=1, device_id=device(lax.rem(index + d, count)), device_id_type=MESH)
        greeted = greeted + (count - 1)

    loads = []
    for t in range(step):
        mine_at, other_at = pl.ds(start_of(member), cw), pl.ds(start_of(1 - member), cw)
        loads.append((clip.at[t, :, other_at], cross.at[t]))
        loads.append((clip.at[t, :, mine_at], pads.at[0, HALO + step * member + t, pl.ds(1, rows)]))
    loads.append((w1, w1v))
    loads.append((w2, w2v))
    for t in range(step):
        loads.append((cot.at[t, :, mine_at], cotp.at[step * member + t]))
    loads = [pltpu.make_async_copy(a, b, l_sem.at[i]) for i, (a, b) in enumerate(loads)]
    for load in loads:
        load.start()

    def zero(ref):
        ref[...] = jnp.zeros(ref.shape, ref.dtype)

    for k in range(4):
        @pl.when(jnp.logical_not(earlier if k < 2 else later))
        def _():
            for f in ((0, 1) if k < 2 else (frames, frames + 1)):
                zero(pads.at[k, f])

        @pl.when(jnp.logical_not(above))
        def _():
            for f in range(frames + HALO):
                zero(pads.at[k, f, 0])

        @pl.when(jnp.logical_not(below))
        def _():
            for f in range(frames + HALO):
                zero(pads.at[k, f, rows + 1])
    used = 27 * ch
    for i in range(2):
        mine[i, pl.ds(used, mine.shape[1] - used)] = jnp.zeros((mine.shape[1] - used, ch), BF16)

    pl.semaphore_wait(barrier, greeted)

    def remote(src, dst, send, recv, who):
        return pltpu.make_async_remote_copy(
            src_ref=src, dst_ref=dst, send_sem=send, recv_sem=recv, device_id=who, device_id_type=MESH
        )

    def cross_copy(i, t):
        if i == 0:
            src, dst = cross.at[t], pads.at[0, HALO + step * member + t, pl.ds(1, rows)]
        else:
            src, dst = cot.at[t, :, pl.ds(start_of(1 - member), cw)], cotp.at[step * member + t]
        return remote(src, dst, x_send.at[i, t], x_recv.at[i, t], partner)

    def out_copy(i, t):
        src, dst = ((crit_s, critic), (cg_s, clip_grad))[i]
        return remote(
            src.at[step * (1 - member) + t, :, pl.ds(own, half)],
            dst.at[t, :, pl.ds(pl.multiple_of(member * half, half), half)],
            o_send.at[i, t], o_recv.at[i, t], partner,
        )

    def keep_copy(i, t):
        src, dst = ((crit_s, critic), (cg_s, clip_grad))[i]
        return pltpu.make_async_copy(
            src.at[step * member + t, :, pl.ds(own, half)],
            dst.at[t, :, pl.ds(pl.multiple_of(member * half, half), half)],
            l_sem.at[i * step + t],
        )

    def frame_copy(k, t):
        fwd = k < 2
        src, dst = (frames + t, t) if fwd else (t, frames + t)
        return remote(
            pads.at[k, src, pl.ds(1, rows)], pads.at[k, dst, pl.ds(1, rows)],
            f_send.at[k, t], f_recv.at[k, t], {"frame": me_f + 2 if fwd else me_f - 2},
        )

    def row_copy(k, f, way):
        src, dst = ((rows, 0), (1, rows + 1))[way]
        return remote(
            pads.at[k, f, src], pads.at[k, f, dst],
            r_send.at[k, f, way], r_recv.at[k, f, way], {"row": me_r + 1 if way == 0 else me_r - 1},
        )

    def send_rows(k, f):
        @pl.when(below)
        def _():
            row_copy(k, f, 0).start()

        @pl.when(above)
        def _():
            row_copy(k, f, 1).start()

    def wait_rows(k, fs):
        for f in fs:
            @pl.when(above)
            def _():
                row_copy(k, f, 0).wait_recv()

            @pl.when(below)
            def _():
                row_copy(k, f, 1).wait_recv()

    def send_frame(k, t):
        @pl.when(later if k < 2 else earlier)
        def _():
            frame_copy(k, t).start()

    def take_halo(k):
        fwd = k < 2

        @pl.when(earlier if fwd else later)
        def _():
            for t in ((1, 0) if fwd else (0, 1)):
                frame_copy(k, t).wait_recv()
                send_rows(k, t if fwd else frames + t)
            wait_rows(k, (1, 0) if fwd else (frames, frames + 1))

    def spans():
        lo, size, out = 0, mine.shape[1], []
        for count, index, _ in groups:
            size //= count
            lo = lo + index * size
            out.append((lo, size))
        return out

    parts = spans()

    def scatter_copy(i, level, d):
        count, index, device = groups[level]
        size = parts[level][1]
        src = (mine.at[i], sum_a.at[i], sum_b.at[i])[level]
        peer = lax.rem(index + d, count)
        return remote(
            src.at[pl.ds(pl.multiple_of(peer * size, 16), size)],
            (land_a, land_b, land_c)[level].at[i, d - 1],
            s_send.at[i, level, d - 1], s_recv.at[i, level, d - 1], device(peer),
        )

    def scatter_start(i, level):
        for d in range(1, groups[level][0]):
            scatter_copy(i, level, d).start()

    def scatter_end(i, level):
        count, index, _ = groups[level]
        lo, size = parts[level]
        for d in range(1, count):
            scatter_copy(i, level, d).wait_recv()
        src = (mine.at[i], sum_a.at[i], sum_b.at[i])[level]
        land = (land_a, land_b, land_c)[level]
        z = src[pl.ds(pl.multiple_of(index * size, 16), size)].astype(F32)
        for d in range(1, count):
            z = z + land[i, d - 1].astype(F32)
        if level < 2:
            (sum_a, sum_b)[level][i] = z.astype(BF16)
        else:
            (total1, total2)[i][pl.ds(pl.multiple_of(lo, 16), size)] = z.astype(BF16)

    def gather_copy(i, level, d):
        count, index, device = groups[level]
        lo, size = parts[level]
        part = (total1, total2)[i].at[pl.ds(pl.multiple_of(lo, 16), size)]
        return remote(
            part, part, t_send.at[i, level, d - 1], t_recv.at[i, level, d - 1], device(lax.rem(index + d, count))
        )

    def gather_start(i, level):
        for d in range(1, groups[level][0]):
            gather_copy(i, level, d).start()

    def gather_end(i, level):
        for d in range(1, groups[level][0]):
            gather_copy(i, level, d).wait_recv()

    def shifted(p):
        left, mid, right = (p[:, c * ch : (c + 1) * ch].reshape(rows, cw, ch) for c in range(3))
        pos = lax.broadcasted_iota(jnp.int32, (rows, cw, ch), 1)
        return (
            jnp.where(pos == 0, 0.0, pltpu.roll(left, 1, 1)) + mid
            + jnp.where(pos == cw - 1, 0.0, pltpu.roll(right, cw - 1, 1))
        )

    def conv_pair(k, w, t, epilogue):
        def x(j, b):
            return pads[k, t + j, pl.ds(b, rows)].reshape(rows * cw, ch)

        def taps(a, b):
            return jnp.concatenate([w[a, b, c] for c in range(3)], axis=1)

        def both(j, b):
            return jnp.concatenate([taps(j, b), taps(j - 1, b)], axis=1)

        def dot(xs, ws):
            return jnp.dot(
                jnp.concatenate(xs, axis=1), jnp.concatenate(ws, axis=0), preferred_element_type=F32
            )

        mid = [(j, b) for j in (1, 2) for b in range(3)]
        p = dot([x(j, b) for j, b in mid], [both(j, b) for j, b in mid])
        q0 = dot([x(0, b) for b in range(3)], [taps(0, b) for b in range(3)])
        q1 = dot([x(3, b) for b in range(3)], [taps(2, b) for b in range(3)])
        epilogue(t, shifted(p[:, : 3 * ch] + q0))
        epilogue(t + 1, shifted(p[:, 3 * ch :] + q1))

    inner = pl.ds(1, rows)

    def end0(t, z):
        sigma = jax.nn.sigmoid(z)
        slope1[t] = sigma * (1.0 + z * (1.0 - sigma))
        pads[1, HALO + t, inner] = (z * sigma).astype(BF16)

    def end1(t, z):
        sigma = jax.nn.sigmoid(z)
        crit_s[t] = (z * sigma).astype(BF16)
        delta = cotp[t].astype(F32) * (sigma * (1.0 + z * (1.0 - sigma)))
        pads[2, t, inner] = delta.astype(BF16)

    def end2(t, z):
        pads[3, t, inner] = (z * slope1[t]).astype(BF16)

    def end3(t, z):
        cg_s[t] = z.astype(BF16)

    def turn_weights():
        def one(i, c):
            a, b = i // 3, lax.rem(i, 3)
            for src, dst in ((w1v, w1t), (w2v, w2t)):
                for q in range(3):
                    dst[a, b, q] = src[2 - a, 2 - b, 2 - q].T
            return c
        lax.fori_loop(0, 9, one, 0)

    def turn_input(k, lo, n):
        def one(f, c):
            for r in range(rows + 2):
                xt[k, f, :, r * half : (r + 1) * half] = pads[k, f, r, pl.ds(own, half)].T
            return c
        lax.fori_loop(lo, lo + n, one, 0)

    def spread_delta(k, lo, n):
        def one(t, c):
            pos = lax.broadcasted_iota(jnp.int32, (cw, ch), 0)
            for r in range(rows):
                x = pads[k, t, r + 1].astype(F32)
                d3[t, r, :, 0:ch] = jnp.where(pos == cw - 1, 0.0, pltpu.roll(x, cw - 1, 0)).astype(BF16)
                d3[t, r, :, ch : 2 * ch] = pads[k, t, r + 1]
                d3[t, r, :, 2 * ch :] = jnp.where(pos == 0, 0.0, pltpu.roll(x, 1, 0)).astype(BF16)
            return c
        lax.fori_loop(lo, lo + n, one, 0)

    def weight_grad(k, ts, last, i):
        def one(a, c):
            z = None
            for t in ts:
                x = xt[k, t + a]
                left = jnp.concatenate([x[:, b * half : (b + rows) * half] for b in range(3)], axis=0)
                right = d3[t, :, pl.ds(own, half)].reshape(rows * half, 3 * ch)
                p = jnp.dot(left, right, preferred_element_type=F32)
                z = p if z is None else z + p
            if not last:
                acc[a] = z
            else:
                z = (z + acc[a]) * grad_scale
                for b in range(3):
                    for q in range(3):
                        at = pl.multiple_of(a * (9 * ch) + (b * 3 + q) * ch, ch)
                        mine[i, pl.ds(at, ch)] = z[b * ch : (b + 1) * ch, q * ch : (q + 1) * ch].astype(BF16)
            return c
        lax.fori_loop(0, 3, one, 0)

    for t in range(step):
        loads[2 * t].wait()
    for t in (1, 0):
        cross_copy(0, t).start()
    for t in range(step):
        loads[2 * t + 1].wait()

    def publish_clip(who, fs):
        @pl.when(who)
        def _():
            for f in fs:
                if f >= frames:
                    send_frame(0, f - frames)
                send_rows(0, f)

    publish_clip(second, (frames + 1, frames))
    publish_clip(first, (HALO + 1, HALO))
    for t in (1, 0):
        cross_copy(1, t).start()
    loads[2 * step].wait()
    loads[2 * step + 1].wait()
    turn_weights()
    for t in (1, 0):
        cross_copy(0, t).wait_recv()
        publish_clip(first, (HALO + step + t,))
        publish_clip(second, (HALO + t,))

    local_f = tuple(range(HALO, HALO + frames))
    local_b = tuple(range(frames))

    wait_rows(0, local_f)
    conv_pair(0, w1v, 2, end0)
    for t in (1, 0):
        send_frame(1, t)
        send_rows(1, frames + t)
    take_halo(0)
    conv_pair(0, w1v, 0, end0)
    for f in (HALO + 1, HALO):
        send_rows(1, f)
    turn_input(0, 0, frames + HALO)

    for t in range(step):
        loads[2 * step + 2 + t].wait()
        cross_copy(1, t).wait_recv()
    wait_rows(1, local_f)
    conv_pair(1, w2v, 2, end1)
    for t in (2, 3):
        send_rows(2, t)

    def send_out(i, who):
        @pl.when(who)
        def _():
            for t in range(step):
                out_copy(i, t).start()

    send_out(0, first)
    turn_input(1, HALO, frames)
    spread_delta(2, 2, 2)
    weight_grad(1, (2, 3), False, 1)
    take_halo(1)
    conv_pair(1, w2v, 0, end1)
    for t in (0, 1):
        send_frame(2, t)
        send_rows(2, t)
    send_out(0, second)
    for t in range(step):
        keep_copy(0, t).start()
    turn_input(1, 0, HALO)
    spread_delta(2, 0, 2)
    weight_grad(1, (0, 1), True, 1)
    scatter_start(1, 0)

    wait_rows(2, local_b)
    conv_pair(2, w2t, 0, end2)
    for t in (0, 1):
        send_frame(3, t)
        send_rows(3, t)
    scatter_end(1, 0)
    scatter_start(1, 1)
    spread_delta(3, 0, 2)
    weight_grad(0, (0, 1), False, 0)
    take_halo(2)
    conv_pair(2, w2t, 2, end2)
    for t in (2, 3):
        send_rows(3, t)
    spread_delta(3, 2, 2)
    weight_grad(0, (2, 3), True, 0)
    scatter_start(0, 0)
    scatter_end(1, 1)
    scatter_start(1, 2)

    wait_rows(3, local_b)
    scatter_end(0, 0)
    scatter_start(0, 1)
    conv_pair(3, w1t, 0, end3)
    send_out(1, second)
    scatter_end(1, 2)
    gather_start(1, 2)
    take_halo(3)
    conv_pair(3, w1t, 2, end3)
    send_out(1, first)
    for t in range(step):
        keep_copy(1, t).start()
    scatter_end(0, 1)
    scatter_start(0, 2)
    gather_end(1, 2)
    gather_start(1, 1)
    scatter_end(0, 2)
    gather_start(0, 2)
    gather_end(1, 1)
    gather_start(1, 0)
    gather_end(0, 2)
    gather_start(0, 1)
    gather_end(1, 0)
    gather_end(0, 1)
    gather_start(0, 0)
    gather_end(0, 0)

    for i in range(2):
        for t in range(step):
            cross_copy(i, t).wait_send()
            out_copy(i, t).wait()
            keep_copy(i, t).wait()
        for level in range(3):
            for d in range(1, groups[level][0]):
                scatter_copy(i, level, d).wait_send()
                gather_copy(i, level, d).wait_send()
    for k in range(4):
        fwd = k < 2

        @pl.when(later if fwd else earlier)
        def _():
            for t in range(HALO):
                frame_copy(k, t).wait_send()
        for f in range(frames + HALO):
            is_halo = f < HALO if fwd else f >= frames
            has = earlier if fwd else later
            for way, there in ((0, below), (1, above)):
                @pl.when(jnp.logical_and(there, has) if is_halo else there)
                def _():
                    row_copy(k, f, way).wait_send()


def on_device(n_frame, n_row, clip, first_kernel, second_kernel, cotangent):
    step, rows, width, ch = clip.shape
    grad_scale = 1.0 / float(step * n_frame * rows * n_row * width) ** 0.5
    n = n_frame * n_row
    frames, cw = 2 * step, width // 2 + MARGIN
    vmem, hbm = pl.BlockSpec(memory_space=pltpu.VMEM), pl.BlockSpec(memory_space=pl.ANY)
    weights = first_kernel.shape
    length = 27 * ch
    padded = -(-length // (16 * n)) * 16 * n
    counts = (2, n_row // 2 * 2, n_frame // 2)
    size_a = padded // counts[0]
    size_b = size_a // counts[1]
    size_c = size_b // counts[2]
    most = max(counts) - 1
    sems = pltpu.SemaphoreType.DMA
    block = (frames, rows, cw, ch)
    critic, clip_grad, t1, t2 = pl.pallas_call(
        functools.partial(kernel, n_frame, n_row, grad_scale),
        out_shape=(
            jax.ShapeDtypeStruct(clip.shape, BF16),
            jax.ShapeDtypeStruct(clip.shape, BF16),
            jax.ShapeDtypeStruct((padded, ch), BF16),
            jax.ShapeDtypeStruct((padded, ch), BF16),
        ),
        in_specs=[hbm] * 4,
        out_specs=(hbm, hbm, vmem, vmem),
        scratch_shapes=[
            pltpu.VMEM((4, frames + HALO, rows + 2, cw, ch), BF16),
            pltpu.VMEM((step, rows, cw, ch), BF16),
            pltpu.VMEM(block, BF16),
            pltpu.VMEM(block, BF16),
            pltpu.VMEM(block, BF16),
            pltpu.VMEM(block, F32),
            pltpu.VMEM(weights, BF16),
            pltpu.VMEM(weights, BF16),
            pltpu.VMEM(weights, BF16),
            pltpu.VMEM(weights, BF16),
            pltpu.VMEM((2, frames + HALO, ch, (rows + 2) * (width // 2)), BF16),
            pltpu.VMEM((frames, rows, cw, 3 * ch), BF16),
            pltpu.VMEM((3, 3 * ch, 3 * ch), F32),
            pltpu.VMEM((2, padded, ch), BF16),
            pltpu.VMEM((2, counts[0] - 1, size_a, ch), BF16),
            pltpu.VMEM((2, size_a, ch), BF16),
            pltpu.VMEM((2, counts[1] - 1, size_b, ch), BF16),
            pltpu.VMEM((2, size_b, ch), BF16),
            pltpu.VMEM((2, counts[2] - 1, size_c, ch), BF16),
            sems((3 * step + 2,)),
            sems((2, step)), sems((2, step)),
            sems((2, step)), sems((2, step)),
            sems((4, HALO)), sems((4, HALO)),
            sems((4, frames + HALO, 2)), sems((4, frames + HALO, 2)),
            sems((2, 3, most)), sems((2, 3, most)),
            sems((2, 3, most)), sems((2, 3, most)),
        ],
        compiler_params=pltpu.CompilerParams(
            collective_id=0, has_side_effects=True, vmem_limit_bytes=60 * 2**20
        ),
    )(clip, first_kernel, second_kernel, cotangent)
    g1, g2 = (t[:length].astype(F32).reshape(weights) for t in (t1, t2))
    return critic, clip_grad, g1, g2


def solution(mesh):
    placed = (P("frame", "row", None, None), P(), P(), P("frame", "row", None, None))
    return jax.shard_map(
        functools.partial(on_device, mesh.shape["frame"], mesh.shape["row"]),
        mesh=mesh,
        in_specs=placed,
        out_specs=(P("frame", "row", None, None), P("frame", "row", None, None), P(), P()),
        check_vma=False,
    )
```

time: 143 us -> 86.4 us (0.60)
  Pallas kernels: 136 us -> 79.9 us
  other arithmetic: 4.37 us -> 2.81 us
    pallas_call x1 -> x0, Pallas kernels: 61.7 us -> none  [summed(): pl.pallas_call(functools.partial(sum_kernel, levels, n), out_shape=jax.Sh...]
    pallas_call x1, Pallas kernels: 74.2 us -> 79.9 us  [on_device(): pl.pallas_call(functools.partial(kernel, n_frame, n_row, grad_scale), out...]
    concatenate x1 -> x0, other arithmetic: 1.55 us -> none  [on_device(): flat = jnp.concatenate([g1.reshape(-1, ch), g2.reshape(-1, ch)])]
where the time goes in v1:
time: 86.4 us; the launch traced here: 86.3 us
  Pallas kernels  79.9 us (92%)
  local copies, waits for them, and re-layouts  2.88 us (3%)
  other arithmetic  2.81 us (3%)
    pallas_call x1, Pallas kernels, on_device(): pl.pallas_call(functools.partial(kernel, n_frame, n_row, grad_scale), out...  79.9 us
    reshape x2, other arithmetic, on_device(): g1, g2 = (t[:length].astype(F32).reshape(weights) for t in (t1, t2))  2.81 us

profile of v1, /device:TPU:0, one launch (start us, length us, event | category | flops | bytes accessed | tf_op | source)
XLA Modules:
  0.0 86.3 jit_solution(4233431783761931790)
XLA Ops:
  0.6 79.9 %shard_map.75 = (bf16[2,4,256,128]{3,2,1,0:T(8,128)(2,1)}, bf16[2,4,256,128]{3,2,1,0:T(8,128)(2,1)}, bf16[3584,128]{1,0:T(8,128)(2,1)}, bf16[3584,128]{1,0:T(8,128)(2,1)}) custom-call(bf16[2,4,256,128]{3,2,1,0:T(8,128)(2,1)} %clip.1, bf16[3,3,3,128,128]{4,3,2,1,0:T(8,128)(2,1)} %w1.1, bf16[3,3,3,128,128]{4,3,2,1,0:T(8,128)(2,1)} %w2.1, ...), custom_call_target="tpu_custom_call" | custom-call | tf_op jit(solution)/shard_map/pallas_call | solution.py:486
  80.5 1.2 %slice.6 = bf16[3456,128]{1,0:T(8,128)(2,1)S(1)} slice(bf16[3584,128]{1,0:T(8,128)(2,1)} %get-tuple-element.10), slice={[0:3456], [0:128]} | slice | bytes 1769472 | tf_op jit(solution)/shard_map/slice | solution.py:528
  81.7 0.0 copy-start
  81.8 1.4 %convert.2 = f32[3,3,3,128,128]{4,3,2,1,0:T(8,128)} convert(bf16[3,3,3,128,128]{4,3,2,1,0:T(8,128)(2,1)S(1)} %bitcast.4) | non-fusion elementwise | flops 442368 | bytes 2654208 | tf_op jit(solution)/shard_map/reshape | solution.py:528
  83.2 0.0 copy-done
  83.2 0.1 slice.7
  83.2 0.0 copy-start.2
  83.2 0.0 copy-start.1
  83.2 1.4 %convert.3 = f32[3,3,3,128,128]{4,3,2,1,0:T(8,128)} convert(bf16[3,3,3,128,128]{4,3,2,1,0:T(8,128)(2,1)S(1)} %bitcast.5) | non-fusion elementwise | flops 442368 | bytes 2654208 | tf_op jit(solution)/shard_map/reshape | solution.py:528
  84.7 0.0 copy-done.2
  84.7 0.8 copy.10
  85.5 0.0 copy-done.1
  85.5 0.8 copy.11
Async XLA Ops:
  81.7 1.4 %copy-start = (bf16[3584,128]{1,0:T(8,128)(2,1)S(1)}, bf16[3584,128]{1,0:T(8,128)(2,1)}, u32[]{:S(2)}) copy-start(bf16[3584,128]{1,0:T(8,128)(2,1)} %get-tuple-element.11) | copy-start | bytes 2752516
  83.2 1.4 %copy-start.2 = (bf16[2,4,256,128]{3,2,1,0:T(8,128)(2,1)S(1)}, bf16[2,4,256,128]{3,2,1,0:T(8,128)(2,1)}, u32[]{:S(2)}) copy-start(bf16[2,4,256,128]{3,2,1,0:T(8,128)(2,1)} %get-tuple-element.16) | copy-start | bytes 1572868
  83.2 2.2 %copy-start.1 = (bf16[2,4,256,128]{3,2,1,0:T(8,128)(2,1)S(1)}, bf16[2,4,256,128]{3,2,1,0:T(8,128)(2,1)}, u32[]{:S(2)}) copy-start(bf16[2,4,256,128]{3,2,1,0:T(8,128)(2,1)} %get-tuple-element.17) | copy-start | bytes 1572868

commit v2 on v1

--- a/solution.py
+++ b/solution.py
@@ -29,7 +29,8 @@
     critic, clip_grad, total1, total2,
     pads, cross, cotp, crit_s, cg_s, slope1, w1v, w2v, w1t, w2t, xt, d3, acc,
     mine, land_a, sum_a, land_b, sum_b, land_c,
-    l_sem, x_send, x_recv, o_send, o_recv, f_send, f_recv, r_send, r_recv, s_send, s_recv, t_send, t_recv,
+    l_sem, x_send, x_recv, o_send, o_recv, f_send, f_recv, c_send, c_recv, r_send, r_recv,
+    a_send, a_recv, b_send, b_recv, z_send, z_recv, ga_send, ga_recv, gb_send, gb_recv, gz_send, gz_recv,
 ):
     step, rows, width, ch = clip.shape
     half = width // 2
@@ -43,6 +44,9 @@
     partner = {"frame": me_f + 1 - 2 * member}
     groups = sum_groups(n_frame, n_row, me_f, me_r)
     own = pl.multiple_of(member * MARGIN, MARGIN)
+    odd = lax.rem(me_r, 2)
+    facing = jnp.logical_or(jnp.logical_and(odd == 1, below), jnp.logical_and(odd == 0, above))
+    mate, across = me_r + 1 - 2 * odd, me_r - 1 + 2 * odd
 
     def start_of(who):
         return pl.multiple_of(who * (half - MARGIN), MARGIN)
@@ -53,6 +57,14 @@
         def _():
             pl.semaphore_signal(barrier, inc=1, device_id=who, device_id_type=MESH)
     greeted = below.astype(jnp.int32) + above.astype(jnp.int32)
+    for there, way in ((later, 2), (earlier, -2)):
+        met = jnp.logical_and(there, facing)
+
+        @pl.when(met)
+        def _():
+            who = {"frame": me_f + way, "row": across}
+            pl.semaphore_signal(barrier, inc=1, device_id=who, device_id_type=MESH)
+        greeted = greeted + met.astype(jnp.int32)
     for count, index, device in groups[1:]:
         for d in range(1, count):
             pl.semaphore_signal(barrier, inc=1, device_id=device(lax.rem(index + d, count)), device_id_type=MESH)
@@ -157,76 +169,147 @@
             def _():
                 row_copy(k, f, 1).wait_recv()
 
+    def corner_copy(k, t):
+        fwd = k < 2
+        src, dst = (frames + t, t) if fwd else (t, frames + t)
+        return remote(
+            pads.at[k, src, 1 + odd * (rows - 1)], pads.at[k, dst, (1 - odd) * (rows + 1)],
+            c_send.at[k, t], c_recv.at[k, t], {"frame": me_f + 2 if fwd else me_f - 2, "row": across},
+        )
+
+    def mate_copy(k, t):
+        f = t if k < 2 else frames + t
+        return remote(
+            pads.at[k, f, rows - odd * (rows - 1)], pads.at[k, f, odd * (rows + 1)],
+            r_send.at[k, f, 0], r_recv.at[k, f, 0], {"row": mate},
+        )
+
     def send_frame(k, t):
-        @pl.when(later if k < 2 else earlier)
+        there = later if k < 2 else earlier
+
+        @pl.when(there)
         def _():
             frame_copy(k, t).start()
 
-    def take_halo(k):
-        fwd = k < 2
-
-        @pl.when(earlier if fwd else later)
-        def _():
-            for t in ((1, 0) if fwd else (0, 1)):
-                frame_copy(k, t).wait_recv()
-                send_rows(k, t if fwd else frames + t)
-            wait_rows(k, (1, 0) if fwd else (frames, frames + 1))
-
-    def spans():
-        lo, size, out = 0, mine.shape[1], []
-        for count, index, _ in groups:
-            size //= count
-            lo = lo + index * size
-            out.append((lo, size))
-        return out
-
-    parts = spans()
-
-    def scatter_copy(i, level, d):
-        count, index, device = groups[level]
-        size = parts[level][1]
-        src = (mine.at[i], sum_a.at[i], sum_b.at[i])[level]
-        peer = lax.rem(index + d, count)
+        @pl.when(jnp.logical_and(there, facing))
+        def _():
+            corner_copy(k, t).start()
+
+    def pass_halo(k, t):
+        @pl.when(earlier if k < 2 else later)
+        def _():
+            frame_copy(k, t).wait_recv()
+            mate_copy(k, t).start()
+
+    def wait_halo(k):
+        there = earlier if k < 2 else later
+
+        @pl.when(there)
+        def _():
+            for t in range(HALO):
+                mate_copy(k, t).wait_recv()
+
+        @pl.when(jnp.logical_and(there, facing))
+        def _():
+            for t in range(HALO):
+                corner_copy(k, t).wait_recv()
+
+    (_, core, to_core), (n_b, in_b, to_b), (n_c, in_c, to_c) = groups
+    half_rows = sum_a.shape[1]
+    piece = half_rows // (n_b * n_c)
+
+    def aligned(x):
+        return pl.multiple_of(x, 16)
+
+    def block(q):
+        return aligned(q * (n_b * piece))
+
+    def a_copy(i):
+        src = mine.at[i, pl.ds(aligned((1 - core) * half_rows), half_rows)]
+        return remote(src, land_a.at[i], a_send.at[i], a_recv.at[i], to_core(1 - core))
+
+    def b_copy(i, d, e):
+        peer = lax.rem(in_b + e, n_b)
+        src = sum_a.at[i, pl.ds(aligned(block(lax.rem(in_c + d, n_c)) + peer * piece), piece)]
+        return remote(src, land_b.at[i, d, e - 1], b_send.at[i, d, e - 1], b_recv.at[i, d, e - 1], to_b(peer))
+
+    def z_copy(i, d):
+        peer = lax.rem(in_c + d, n_c)
+        return remote(sum_b.at[i, d - 1], land_c.at[i, d - 1], z_send.at[i, d - 1], z_recv.at[i, d - 1], to_c(peer))
+
+    order = tuple(range(n_c - 1, 0, -1))
+
+    def sum_phase_a(i):
+        a_copy(i).start()
+
+    def sum_phase_b(i):
+        a_copy(i).wait_recv()
+        kept = mine[i, pl.ds(aligned(core * half_rows), half_rows)].astype(F32)
+        sum_a[i] = (kept + land_a[i].astype(F32)).astype(BF16)
+        for d in order + (0,):
+            for e in range(1, n_b):
+                b_copy(i, d, e).start()
+
+    def plane_sum(i, d):
+        for e in range(1, n_b):
+            b_copy(i, d, e).wait_recv()
+        z = sum_a[i, pl.ds(aligned(block(lax.rem(in_c + d, n_c)) + in_b * piece), piece)].astype(F32)
+        for e in range(1, n_b):
+            z = z + land_b[i, d, e - 1].astype(F32)
+        return z
+
+    def sum_phase_c(i, ds):
+        for d in ds:
+            sum_b[i, d - 1] = plane_sum(i, d).astype(BF16)
+            z_copy(i, d).start()
+
+    def total_at(i, q, j, n):
+        lo = aligned(core * half_rows + block(q) + j * piece)
+        return (total1, total2)[i].at[pl.ds(lo, n)]
+
+    def gz_copy(i, d):
+        part = total_at(i, in_c, in_b, piece)
+        return remote(part, part, gz_send.at[i, d - 1], gz_recv.at[i, d - 1], to_c(lax.rem(in_c + d, n_c)))
+
+    def source(d):
+        return lax.rem(in_c + n_c - d, n_c)
+
+    def gb_copy(i, d, e):
+        part = total_at(i, source(d), in_b, piece)
         return remote(
-            src.at[pl.ds(pl.multiple_of(peer * size, 16), size)],
-            (land_a, land_b, land_c)[level].at[i, d - 1],
-            s_send.at[i, level, d - 1], s_recv.at[i, level, d - 1], device(peer),
-        )
-
-    def scatter_start(i, level):
-        for d in range(1, groups[level][0]):
-            scatter_copy(i, level, d).start()
-
-    def scatter_end(i, level):
-        count, index, _ = groups[level]
-        lo, size = parts[level]
-        for d in range(1, count):
-            scatter_copy(i, level, d).wait_recv()
-        src = (mine.at[i], sum_a.at[i], sum_b.at[i])[level]
-        land = (land_a, land_b, land_c)[level]
-        z = src[pl.ds(pl.multiple_of(index * size, 16), size)].astype(F32)
-        for d in range(1, count):
-            z = z + land[i, d - 1].astype(F32)
-        if level < 2:
-            (sum_a, sum_b)[level][i] = z.astype(BF16)
-        else:
-            (total1, total2)[i][pl.ds(pl.multiple_of(lo, 16), size)] = z.astype(BF16)
-
-    def gather_copy(i, level, d):
-        count, index, device = groups[level]
-        lo, size = parts[level]
-        part = (total1, total2)[i].at[pl.ds(pl.multiple_of(lo, 16), size)]
-        return remote(
-            part, part, t_send.at[i, level, d - 1], t_recv.at[i, level, d - 1], device(lax.rem(index + d, count))
-        )
-
-    def gather_start(i, level):
-        for d in range(1, groups[level][0]):
-            gather_copy(i, level, d).start()
-
-    def gather_end(i, level):
-        for d in range(1, groups[level][0]):
-            gather_copy(i, level, d).wait_recv()
+            part, part, gb_send.at[i, d, e - 1], gb_recv.at[i, d, e - 1], to_b(lax.rem(in_b + e, n_b))
+        )
+
+    def ga_copy(i, d):
+        part = total_at(i, source(d), 0, n_b * piece)
+        return remote(part, part, ga_send.at[i, d], ga_recv.at[i, d], to_core(1 - core))
+
+    def total_phase_z(i):
+        z = plane_sum(i, 0)
+        for d in range(1, n_c):
+            z_copy(i, d).wait_recv()
+            z = z + land_c[i, d - 1].astype(F32)
+        total_at(i, in_c, in_b, piece)[...] = z.astype(BF16)
+        for d in order:
+            gz_copy(i, d).start()
+        for e in range(1, n_b):
+            gb_copy(i, 0, e).start()
+
+    def total_phase_b(i):
+        for d in range(1, n_c):
+            gz_copy(i, d).wait_recv()
+            for e in range(1, n_b):
+                gb_copy(i, d, e).start()
+
+    def total_phase_a(i):
+        for d in range(n_c):
+            for e in range(1, n_b):
+                gb_copy(i, d, e).wait_recv()
+            ga_copy(i, d).start()
+
+    def total_phase_end(i):
+        for d in range(n_c):
+            ga_copy(i, d).wait_recv()
 
     def shifted(p):
         left, mid, right = (p[:, c * ch : (c + 1) * ch].reshape(rows, cw, ch) for c in range(3))
@@ -359,7 +442,9 @@
     for t in (1, 0):
         send_frame(1, t)
         send_rows(1, frames + t)
-    take_halo(0)
+    pass_halo(0, 1)
+    pass_halo(0, 0)
+    wait_halo(0)
     conv_pair(0, w1v, 0, end0)
     for f in (HALO + 1, HALO):
         send_rows(1, f)
@@ -369,6 +454,7 @@
         loads[2 * step + 2 + t].wait()
         cross_copy(1, t).wait_recv()
     wait_rows(1, local_f)
+    pass_halo(1, 1)
     conv_pair(1, w2v, 2, end1)
     for t in (2, 3):
         send_rows(2, t)
@@ -380,10 +466,11 @@
                 out_copy(i, t).start()
 
     send_out(0, first)
+    pass_halo(1, 0)
     turn_input(1, HALO, frames)
     spread_delta(2, 2, 2)
     weight_grad(1, (2, 3), False, 1)
-    take_halo(1)
+    wait_halo(1)
     conv_pair(1, w2v, 0, end1)
     for t in (0, 1):
         send_frame(2, t)
@@ -394,63 +481,63 @@
     turn_input(1, 0, HALO)
     spread_delta(2, 0, 2)
     weight_grad(1, (0, 1), True, 1)
-    scatter_start(1, 0)
+    sum_phase_a(1)
 
     wait_rows(2, local_b)
     conv_pair(2, w2t, 0, end2)
     for t in (0, 1):
         send_frame(3, t)
         send_rows(3, t)
-    scatter_end(1, 0)
-    scatter_start(1, 1)
+    sum_phase_b(1)
+    pass_halo(2, 0)
     spread_delta(3, 0, 2)
     weight_grad(0, (0, 1), False, 0)
-    take_halo(2)
+    pass_halo(2, 1)
+    sum_phase_c(1, order[:1])
+    wait_halo(2)
     conv_pair(2, w2t, 2, end2)
     for t in (2, 3):
         send_rows(3, t)
+    sum_phase_c(1, order[1:])
     spread_delta(3, 2, 2)
     weight_grad(0, (2, 3), True, 0)
-    scatter_start(0, 0)
-    scatter_end(1, 1)
-    scatter_start(1, 2)
-
+    sum_phase_a(0)
+    total_phase_z(1)
+
+    pass_halo(3, 0)
+    pass_halo(3, 1)
+    sum_phase_b(0)
+    total_phase_b(1)
     wait_rows(3, local_b)
-    scatter_end(0, 0)
-    scatter_start(0, 1)
     conv_pair(3, w1t, 0, end3)
     send_out(1, second)
-    scatter_end(1, 2)
-    gather_start(1, 2)
-    take_halo(3)
+    wait_halo(3)
     conv_pair(3, w1t, 2, end3)
     send_out(1, first)
     for t in range(step):
         keep_copy(1, t).start()
-    scatter_end(0, 1)
-    scatter_start(0, 2)
-    gather_end(1, 2)
-    gather_start(1, 1)
-    scatter_end(0, 2)
-    gather_start(0, 2)
-    gather_end(1, 1)
-    gather_start(1, 0)
-    gather_end(0, 2)
-    gather_start(0, 1)
-    gather_end(1, 0)
-    gather_end(0, 1)
-    gather_start(0, 0)
-    gather_end(0, 0)
+    sum_phase_c(0, order)
+    total_phase_z(0)
+    total_phase_a(1)
+    total_phase_b(0)
+    total_phase_a(0)
+    total_phase_end(1)
+    total_phase_end(0)
 
     for i in range(2):
         for t in range(step):
             cross_copy(i, t).wait_send()
             out_copy(i, t).wait()
             keep_copy(i, t).wait()
-        for level in range(3):
-            for d in range(1, groups[level][0]):
-                scatter_copy(i, level, d).wait_send()
-                gather_copy(i, level, d).wait_send()
+        a_copy(i).wait_send()
+        for d in range(n_c):
+            ga_copy(i, d).wait_send()
+            for e in range(1, n_b):
+                b_copy(i, d, e).wait_send()
+                gb_copy(i, d, e).wait_send()
+        for d in range(1, n_c):
+            z_copy(i, d).wait_send()
+            gz_copy(i, d).wait_send()
     for k in range(4):
         fwd = k < 2
 
@@ -458,11 +545,19 @@
         def _():
             for t in range(HALO):
                 frame_copy(k, t).wait_send()
-        for f in range(frames + HALO):
-            is_halo = f < HALO if fwd else f >= frames
-            has = earlier if fwd else later
+
+        @pl.when(jnp.logical_and(later if fwd else earlier, facing))
+        def _():
+            for t in range(HALO):
+                corner_copy(k, t).wait_send()
+
+        @pl.when(earlier if fwd else later)
+        def _():
+            for t in range(HALO):
+                mate_copy(k, t).wait_send()
+        for f in local_f if fwd else local_b:
             for way, there in ((0, below), (1, above)):
-                @pl.when(jnp.logical_and(there, has) if is_halo else there)
+                @pl.when(there)
                 def _():
                     row_copy(k, f, way).wait_send()
 
@@ -478,9 +573,7 @@
     padded = -(-length // (16 * n)) * 16 * n
     counts = (2, n_row // 2 * 2, n_frame // 2)
     size_a = padded // counts[0]
-    size_b = size_a // counts[1]
-    size_c = size_b // counts[2]
-    most = max(counts) - 1
+    piece = size_a // (counts[1] * counts[2])
     sems = pltpu.SemaphoreType.DMA
     block = (frames, rows, cw, ch)
     critic, clip_grad, t1, t2 = pl.pallas_call(
@@ -508,18 +601,23 @@
             pltpu.VMEM((frames, rows, cw, 3 * ch), BF16),
             pltpu.VMEM((3, 3 * ch, 3 * ch), F32),
             pltpu.VMEM((2, padded, ch), BF16),
-            pltpu.VMEM((2, counts[0] - 1, size_a, ch), BF16),
             pltpu.VMEM((2, size_a, ch), BF16),
-            pltpu.VMEM((2, counts[1] - 1, size_b, ch), BF16),
-            pltpu.VMEM((2, size_b, ch), BF16),
-            pltpu.VMEM((2, counts[2] - 1, size_c, ch), BF16),
+            pltpu.VMEM((2, size_a, ch), BF16),
+            pltpu.VMEM((2, counts[2], counts[1] - 1, piece, ch), BF16),
+            pltpu.VMEM((2, counts[2] - 1, piece, ch), BF16),
+            pltpu.VMEM((2, counts[2] - 1, piece, ch), BF16),
             sems((3 * step + 2,)),
             sems((2, step)), sems((2, step)),
             sems((2, step)), sems((2, step)),
             sems((4, HALO)), sems((4, HALO)),
+            sems((4, HALO)), sems((4, HALO)),
             sems((4, frames + HALO, 2)), sems((4, frames + HALO, 2)),
-            sems((2, 3, most)), sems((2, 3, most)),
-            sems((2, 3, most)), sems((2, 3, most)),
+            sems((2,)), sems((2,)),
+            sems((2, counts[2], counts[1] - 1)), sems((2, counts[2], counts[1] - 1)),
+            sems((2, counts[2] - 1)), sems((2, counts[2] - 1)),
+            sems((2, counts[2])), sems((2, counts[2])),
+            sems((2, counts[2], counts[1] - 1)), sems((2, counts[2], counts[1] - 1)),
+            sems((2, counts[2] - 1)), sems((2, counts[2] - 1)),
         ],
         compiler_params=pltpu.CompilerParams(
             collective_id=0, has_side_effects=True, vmem_limit_bytes=60 * 2**20

time: 86.4 us -> 78.9 us (0.913)
  Pallas kernels: 79.9 us -> 72.4 us
    pallas_call x1, Pallas kernels: 79.9 us -> 72.4 us  [on_device(): pl.pallas_call(functools.partial(kernel, n_frame, n_row, grad_scale), out...]
where the time goes in v2:
time: 78.9 us; the launch traced here: 78.8 us
  Pallas kernels  72.4 us (92%)
  local copies, waits for them, and re-layouts  2.88 us (4%)
  other arithmetic  2.81 us (4%)
    pallas_call x1, Pallas kernels, on_device(): pl.pallas_call(functools.partial(kernel, n_frame, n_row, grad_scale), out...  72.4 us
    reshape x2, other arithmetic, on_device(): g1, g2 = (t[:length].astype(F32).reshape(weights) for t in (t1, t2))  2.81 us
    unnamed x8, local copies, waits for them, and re-layouts  1.6 us

profile of v2, /device:TPU:0, one launch (start us, length us, event | category | flops | bytes accessed | tf_op | source)
XLA Modules:
  0.0 78.8 jit_solution(4411200547159339661)
XLA Ops:
  0.6 72.4 %shard_map.75 = (bf16[2,4,256,128]{3,2,1,0:T(8,128)(2,1)}, bf16[2,4,256,128]{3,2,1,0:T(8,128)(2,1)}, bf16[3584,128]{1,0:T(8,128)(2,1)}, bf16[3584,128]{1,0:T(8,128)(2,1)}) custom-call(bf16[2,4,256,128]{3,2,1,0:T(8,128)(2,1)} %clip.1, bf16[3,3,3,128,128]{4,3,2,1,0:T(8,128)(2,1)} %w1.1, bf16[3,3,3,128,128]{4,3,2,1,0:T(8,128)(2,1)} %w2.1, ...), custom_call_target="tpu_custom_call" | custom-call | tf_op jit(solution)/shard_map/pallas_call | solution.py:579
  73.0 1.2 %slice.6 = bf16[3456,128]{1,0:T(8,128)(2,1)S(1)} slice(bf16[3584,128]{1,0:T(8,128)(2,1)} %get-tuple-element.10), slice={[0:3456], [0:128]} | slice | bytes 1769472 | tf_op jit(solution)/shard_map/slice | solution.py:626
  74.3 0.0 copy-start
  74.3 1.4 %convert.2 = f32[3,3,3,128,128]{4,3,2,1,0:T(8,128)} convert(bf16[3,3,3,128,128]{4,3,2,1,0:T(8,128)(2,1)S(1)} %bitcast.4) | non-fusion elementwise | flops 442368 | bytes 2654208 | tf_op jit(solution)/shard_map/reshape | solution.py:626
  75.7 0.0 copy-done
  75.7 0.1 slice.7
  75.7 0.0 copy-start.2
  75.7 0.0 copy-start.1
  75.8 1.4 %convert.3 = f32[3,3,3,128,128]{4,3,2,1,0:T(8,128)} convert(bf16[3,3,3,128,128]{4,3,2,1,0:T(8,128)(2,1)S(1)} %bitcast.5) | non-fusion elementwise | flops 442368 | bytes 2654208 | tf_op jit(solution)/shard_map/reshape | solution.py:626
  77.2 0.0 copy-done.2
  77.2 0.8 %copy.10 = bf16[2,4,256,128]{3,2,1,0:T(8,128)(2,1)} copy(bf16[2,4,256,128]{3,2,1,0:T(8,128)(2,1)S(1)} %copy-done.2) | data formatting | bytes 1048576
  78.0 0.0 copy-done.1
  78.0 0.8 %copy.11 = bf16[2,4,256,128]{3,2,1,0:T(8,128)(2,1)} copy(bf16[2,4,256,128]{3,2,1,0:T(8,128)(2,1)S(1)} %copy-done.1) | data formatting | bytes 1048576
Async XLA Ops:
  74.3 1.4 %copy-start = (bf16[3584,128]{1,0:T(8,128)(2,1)S(1)}, bf16[3584,128]{1,0:T(8,128)(2,1)}, u32[]{:S(2)}) copy-start(bf16[3584,128]{1,0:T(8,128)(2,1)} %get-tuple-element.11) | copy-start | bytes 2752516
  75.7 1.4 %copy-start.2 = (bf16[2,4,256,128]{3,2,1,0:T(8,128)(2,1)S(1)}, bf16[2,4,256,128]{3,2,1,0:T(8,128)(2,1)}, u32[]{:S(2)}) copy-start(bf16[2,4,256,128]{3,2,1,0:T(8,128)(2,1)} %get-tuple-element.16) | copy-start | bytes 1572868
  75.7 2.2 %copy-start.1 = (bf16[2,4,256,128]{3,2,1,0:T(8,128)(2,1)S(1)}, bf16[2,4,256,128]{3,2,1,0:T(8,128)(2,1)}, u32[]{:S(2)}) copy-start(bf16[2,4,256,128]{3,2,1,0:T(8,128)(2,1)} %get-tuple-element.17) | copy-start | bytes 1572868

commit v3 on v2

--- a/solution.py
+++ b/solution.py
@@ -14,12 +14,11 @@
 
 
 def sum_groups(n_frame, n_row, me_f, me_r):
-    pair, member = me_f // 2, lax.rem(me_f, 2)
     side, core = me_r // 2, lax.rem(me_r, 2)
     return (
         (2, core, lambda j: {"row": side * 2 + j}),
-        (n_row // 2 * 2, side * 2 + member, lambda j: {"row": j // 2 * 2 + core, "frame": pair * 2 + lax.rem(j, 2)}),
-        (n_frame // 2, pair, lambda j: {"frame": j * 2 + member}),
+        (n_row // 2, side, lambda j: {"row": j * 2 + core}),
+        (n_frame, me_f, lambda j: {"frame": j}),
     )
 
 
@@ -127,13 +126,10 @@
             o_send.at[i, t], o_recv.at[i, t], partner,
         )
 
-    def keep_copy(i, t):
+    def keep(i):
         src, dst = ((crit_s, critic), (cg_s, clip_grad))[i]
-        return pltpu.make_async_copy(
-            src.at[step * member + t, :, pl.ds(own, half)],
-            dst.at[t, :, pl.ds(pl.multiple_of(member * half, half), half)],
-            l_sem.at[i * step + t],
-        )
+        for t in range(step):
+            dst[t, :, pl.ds(pl.multiple_of(member * half, half), half)] = src[step * member + t, :, pl.ds(own, half)]
 
     def frame_copy(k, t):
         fwd = k < 2
@@ -237,7 +233,8 @@
         peer = lax.rem(in_c + d, n_c)
         return remote(sum_b.at[i, d - 1], land_c.at[i, d - 1], z_send.at[i, d - 1], z_recv.at[i, d - 1], to_c(peer))
 
-    order = tuple(range(n_c - 1, 0, -1))
+    near = sorted(range(1, n_c), key=lambda d: min(d, n_c - d))
+    order = tuple(reversed(near))
 
     def sum_phase_a(i):
         a_copy(i).start()
@@ -296,13 +293,13 @@
             gb_copy(i, 0, e).start()
 
     def total_phase_b(i):
-        for d in range(1, n_c):
+        for d in near:
             gz_copy(i, d).wait_recv()
             for e in range(1, n_b):
                 gb_copy(i, d, e).start()
 
     def total_phase_a(i):
-        for d in range(n_c):
+        for d in [0] + near:
             for e in range(1, n_b):
                 gb_copy(i, d, e).wait_recv()
             ga_copy(i, d).start()
@@ -476,8 +473,7 @@
         send_frame(2, t)
         send_rows(2, t)
     send_out(0, second)
-    for t in range(step):
-        keep_copy(0, t).start()
+    keep(0)
     turn_input(1, 0, HALO)
     spread_delta(2, 0, 2)
     weight_grad(1, (0, 1), True, 1)
@@ -493,12 +489,12 @@
     spread_delta(3, 0, 2)
     weight_grad(0, (0, 1), False, 0)
     pass_halo(2, 1)
-    sum_phase_c(1, order[:1])
+    sum_phase_c(1, order[:2])
     wait_halo(2)
     conv_pair(2, w2t, 2, end2)
     for t in (2, 3):
         send_rows(3, t)
-    sum_phase_c(1, order[1:])
+    sum_phase_c(1, order[2:])
     spread_delta(3, 2, 2)
     weight_grad(0, (2, 3), True, 0)
     sum_phase_a(0)
@@ -507,15 +503,14 @@
     pass_halo(3, 0)
     pass_halo(3, 1)
     sum_phase_b(0)
-    total_phase_b(1)
     wait_rows(3, local_b)
     conv_pair(3, w1t, 0, end3)
     send_out(1, second)
     wait_halo(3)
     conv_pair(3, w1t, 2, end3)
     send_out(1, first)
-    for t in range(step):
-        keep_copy(1, t).start()
+    keep(1)
+    total_phase_b(1)
     sum_phase_c(0, order)
     total_phase_z(0)
     total_phase_a(1)
@@ -528,7 +523,6 @@
         for t in range(step):
             cross_copy(i, t).wait_send()
             out_copy(i, t).wait()
-            keep_copy(i, t).wait()
         a_copy(i).wait_send()
         for d in range(n_c):
             ga_copy(i, d).wait_send()
@@ -562,16 +556,35 @@
                     row_copy(k, f, way).wait_send()
 
 
+def finish(t1, t2, critic, clip_grad, g1, g2, critic_out, clip_grad_out, wide, g_sem, o_sem):
+    copies = [
+        pltpu.make_async_copy(src, dst, o_sem.at[i])
+        for i, (src, dst) in enumerate(((critic, critic_out), (clip_grad, clip_grad_out)))
+    ]
+    for copy in copies:
+        copy.start()
+    part = wide.shape[1] // 3
+    for i, (src, dst) in enumerate(((t1, g1), (t2, g2))):
+        for a in range(3):
+            at = pl.ds(a * part, part)
+            wide[i, at] = src[at].astype(F32)
+            copy = pltpu.make_async_copy(wide.at[i, at], dst.at[at], g_sem.at[i, a])
+            copy.start()
+            copies.append(copy)
+    for copy in copies:
+        copy.wait()
+
+
 def on_device(n_frame, n_row, clip, first_kernel, second_kernel, cotangent):
     step, rows, width, ch = clip.shape
     grad_scale = 1.0 / float(step * n_frame * rows * n_row * width) ** 0.5
     n = n_frame * n_row
     frames, cw = 2 * step, width // 2 + MARGIN
-    vmem, hbm = pl.BlockSpec(memory_space=pltpu.VMEM), pl.BlockSpec(memory_space=pl.ANY)
+    vmem, hbm = pl.BlockSpec(memory_space=pltpu.VMEM), pl.BlockSpec(memory_space=pltpu.HBM)
     weights = first_kernel.shape
     length = 27 * ch
     padded = -(-length // (16 * n)) * 16 * n
-    counts = (2, n_row // 2 * 2, n_frame // 2)
+    counts = (2, n_row // 2, n_frame)
     size_a = padded // counts[0]
     piece = size_a // (counts[1] * counts[2])
     sems = pltpu.SemaphoreType.DMA
@@ -585,7 +598,7 @@
             jax.ShapeDtypeStruct((padded, ch), BF16),
         ),
         in_specs=[hbm] * 4,
-        out_specs=(hbm, hbm, vmem, vmem),
+        out_specs=(vmem,) * 4,
         scratch_shapes=[
             pltpu.VMEM((4, frames + HALO, rows + 2, cw, ch), BF16),
             pltpu.VMEM((step, rows, cw, ch), BF16),
@@ -620,11 +633,19 @@
             sems((2, counts[2] - 1)), sems((2, counts[2] - 1)),
         ],
         compiler_params=pltpu.CompilerParams(
-            collective_id=0, has_side_effects=True, vmem_limit_bytes=60 * 2**20
+            collective_id=0, has_side_effects=True, vmem_limit_bytes=32 * 2**20
         ),
-    )(clip, first_kernel, second_kernel, cotangent)
-    g1, g2 = (t[:length].astype(F32).reshape(weights) for t in (t1, t2))
-    return critic, clip_grad, g1, g2
+    )(*(pltpu.with_memory_space_constraint(v, pltpu.HBM) for v in (clip, first_kernel, second_kernel, cotangent)))
+    flat = jax.ShapeDtypeStruct((length, ch), F32)
+    g1, g2, critic, clip_grad = pl.pallas_call(
+        finish,
+        out_shape=(flat, flat, jax.ShapeDtypeStruct(clip.shape, BF16), jax.ShapeDtypeStruct(clip.shape, BF16)),
+        in_specs=[vmem] * 4,
+        out_specs=(hbm,) * 4,
+        scratch_shapes=[pltpu.VMEM((2, length, ch), F32), sems((2, 3)), sems((2,))],
+        compiler_params=pltpu.CompilerParams(vmem_limit_bytes=16 * 2**20),
+    )(t1, t2, critic, clip_grad)
+    return critic, clip_grad, g1.reshape(weights), g2.reshape(weights)
 
 
 def solution(mesh):

time: 78.9 us -> 81.6 us (1.034)
  Pallas kernels: 72.4 us -> 80.7 us
  local copies, waits for them, and re-layouts: 2.88 us -> 0 us
  other arithmetic: 2.81 us -> 0 us
    pallas_call x1, Pallas kernels: 72.4 us -> 78.5 us  [on_device(): pl.pallas_call(functools.partial(kernel, n_frame, n_row, grad_scale), out...]
    reshape x2 -> x0, other arithmetic: 2.81 us -> none  [on_device(): g1, g2 = (t[:length].astype(F32).reshape(weights) for t in (t1, t2))]
    pallas_call x0 -> x1, Pallas kernels: none -> 2.2 us  [on_device(): pl.pallas_call(finish, out_shape=(flat, flat, jax.ShapeDtypeStruct(clip.s...]
    unnamed x8 -> x0, local copies, waits for them, and re-layouts: 1.6 us -> none
    slice x2 -> x0, local copies, waits for them, and re-layouts: 1.28 us -> none  [on_device(): g1, g2 = (t[:length].astype(F32).reshape(weights) for t in (t1, t2))]
where the time goes in v3:
time: 81.6 us; the launch traced here: 81.5 us
  Pallas kernels  80.7 us (99%)
    pallas_call x1, Pallas kernels, on_device(): pl.pallas_call(functools.partial(kernel, n_frame, n_row, grad_scale), out...  78.5 us
    pallas_call x1, Pallas kernels, on_device(): pl.pallas_call(finish, out_shape=(flat, flat, jax.ShapeDtypeStruct(clip.s...  2.2 us

profile of v3, /device:TPU:0, one launch (start us, length us, event | category | flops | bytes accessed | tf_op | source)
XLA Modules:
  0.0 81.5 jit_solution(1180717666130563431)
XLA Ops:
  0.6 78.5 %shard_map.75 = (bf16[2,4,256,128]{3,2,1,0:T(8,128)(2,1)S(1)}, bf16[2,4,256,128]{3,2,1,0:T(8,128)(2,1)S(1)}, bf16[3584,128]{1,0:T(8,128)(2,1)S(1)}, bf16[3584,128]{1,0:T(8,128)(2,1)S(1)}) custom-call(bf16[2,4,256,128]{3,2,1,0:T(8,128)(2,1)} %clip.1, bf16[3,3,3,128,128]{4,3,2,1,0:T(8,128)(2,1)} %w1.1, bf16[3,3,3,128,128]{4,3,2,1,0:T(8,128)(2,1)} %w2.1, ...), custom_call_target="tpu_custom_call" | custom-call | tf_op jit(solution)/shard_map/pallas_call | solution.py:592
  79.1 2.2 %shard_map.76 = (f32[3456,128]{1,0:T(8,128)}, f32[3456,128]{1,0:T(8,128)}, bf16[2,4,256,128]{3,2,1,0:T(8,128)(2,1)}, bf16[2,4,256,128]{3,2,1,0:T(8,128)(2,1)}) custom-call(bf16[3584,128]{1,0:T(8,128)(2,1)S(1)} %get-tuple-element.12.t1, bf16[3584,128]{1,0:T(8,128)(2,1)S(1)} %get-tuple-element.13.t2, bf16[2,4,256,128]{3,2,1,0:T(8,128)(2,1)S(1)} %get-tuple-element.14.critic, ...), custom_call_target="tpu_custom_call" | custom-call | tf_op jit(solution)/shard_map/pallas_call | solution.py:640

commit v4 on v3

--- a/solution.py
+++ b/solution.py
@@ -14,11 +14,12 @@
 
 
 def sum_groups(n_frame, n_row, me_f, me_r):
+    pair, member = me_f // 2, lax.rem(me_f, 2)
     side, core = me_r // 2, lax.rem(me_r, 2)
     return (
         (2, core, lambda j: {"row": side * 2 + j}),
-        (n_row // 2, side, lambda j: {"row": j * 2 + core}),
-        (n_frame, me_f, lambda j: {"frame": j}),
+        (n_row // 2 * 2, side * 2 + member, lambda j: {"row": j // 2 * 2 + core, "frame": pair * 2 + lax.rem(j, 2)}),
+        (n_frame // 2, pair, lambda j: {"frame": j * 2 + member}),
     )
 
 
@@ -281,6 +282,25 @@
         part = total_at(i, source(d), 0, n_b * piece)
         return remote(part, part, ga_send.at[i, d], ga_recv.at[i, d], to_core(1 - core))
 
+    def gx_copy(d):
+        part = total_at(1, source(d), in_b, piece)
+        return remote(part, part, gb_send.at[1, d, 0], gb_recv.at[1, d, 0], partner)
+
+    def gy_copy(d):
+        side = me_r // 2
+        part = total_at(1, source(d), side * 2, 2 * piece)
+        return remote(part, part, gb_send.at[1, d, 1], gb_recv.at[1, d, 1], {"row": me_r + 2 - 4 * side})
+
+    def total_phase_x():
+        for d in near:
+            gz_copy(1, d).wait_recv()
+            gx_copy(d).start()
+
+    def total_phase_y(ds):
+        for d in ds:
+            gx_copy(d).wait_recv()
+            gy_copy(d).start()
+
     def total_phase_z(i):
         z = plane_sum(i, 0)
         for d in range(1, n_c):
@@ -289,8 +309,11 @@
         total_at(i, in_c, in_b, piece)[...] = z.astype(BF16)
         for d in order:
             gz_copy(i, d).start()
-        for e in range(1, n_b):
-            gb_copy(i, 0, e).start()
+        if i == 1:
+            gx_copy(0).start()
+        else:
+            for e in range(1, n_b):
+                gb_copy(i, 0, e).start()
 
     def total_phase_b(i):
         for d in near:
@@ -300,8 +323,11 @@
 
     def total_phase_a(i):
         for d in [0] + near:
-            for e in range(1, n_b):
-                gb_copy(i, d, e).wait_recv()
+            if i == 1:
+                gy_copy(d).wait_recv()
+            else:
+                for e in range(1, n_b):
+                    gb_copy(i, d, e).wait_recv()
             ga_copy(i, d).start()
 
     def total_phase_end(i):
@@ -498,23 +524,26 @@
     spread_delta(3, 2, 2)
     weight_grad(0, (2, 3), True, 0)
     sum_phase_a(0)
-    total_phase_z(1)
 
     pass_halo(3, 0)
     pass_halo(3, 1)
-    sum_phase_b(0)
     wait_rows(3, local_b)
     conv_pair(3, w1t, 0, end3)
-    send_out(1, second)
+    sum_phase_b(0)
+    total_phase_z(1)
     wait_halo(3)
     conv_pair(3, w1t, 2, end3)
+    keep(1)
+    sum_phase_c(0, order[:1])
+    total_phase_x()
+    send_out(1, second)
     send_out(1, first)
-    keep(1)
-    total_phase_b(1)
-    sum_phase_c(0, order)
+    sum_phase_c(0, order[1:])
+    total_phase_y([0] + near[:1])
     total_phase_z(0)
+    total_phase_y(near[1:])
+    total_phase_b(0)
     total_phase_a(1)
-    total_phase_b(0)
     total_phase_a(0)
     total_phase_end(1)
     total_phase_end(0)
@@ -528,7 +557,12 @@
             ga_copy(i, d).wait_send()
             for e in range(1, n_b):
                 b_copy(i, d, e).wait_send()
-                gb_copy(i, d, e).wait_send()
+            if i == 1:
+                gx_copy(d).wait_send()
+                gy_copy(d).wait_send()
+            else:
+                for e in range(1, n_b):
+                    gb_copy(i, d, e).wait_send()
         for d in range(1, n_c):
             z_copy(i, d).wait_send()
             gz_copy(i, d).wait_send()
@@ -584,7 +618,7 @@
     weights = first_kernel.shape
     length = 27 * ch
     padded = -(-length // (16 * n)) * 16 * n
-    counts = (2, n_row // 2, n_frame)
+    counts = (2, n_row // 2 * 2, n_frame // 2)
     size_a = padded // counts[0]
     piece = size_a // (counts[1] * counts[2])
     sems = pltpu.SemaphoreType.DMA

time: 81.6 us -> 71.7 us (0.88)
  Pallas kernels: 80.7 us -> 70.7 us
    pallas_call x1, Pallas kernels: 78.5 us -> 68.5 us  [on_device(): pl.pallas_call(functools.partial(kernel, n_frame, n_row, grad_scale), out...]
where the time goes in v4:
time: 71.7 us; the launch traced here: 71.5 us
  Pallas kernels  70.7 us (99%)
  between operations  0.8 us (1%)
    pallas_call x1, Pallas kernels, on_device(): pl.pallas_call(functools.partial(kernel, n_frame, n_row, grad_scale), out...  68.5 us
    pallas_call x1, Pallas kernels, on_device(): pl.pallas_call(finish, out_shape=(flat, flat, jax.ShapeDtypeStruct(clip.s...  2.2 us

profile of v4, /device:TPU:0, one launch (start us, length us, event | category | flops | bytes accessed | tf_op | source)
XLA Modules:
  0.0 71.5 jit_solution(9113347785389310630)
XLA Ops:
  0.6 68.5 %shard_map.75 = (bf16[2,4,256,128]{3,2,1,0:T(8,128)(2,1)S(1)}, bf16[2,4,256,128]{3,2,1,0:T(8,128)(2,1)S(1)}, bf16[3584,128]{1,0:T(8,128)(2,1)S(1)}, bf16[3584,128]{1,0:T(8,128)(2,1)S(1)}) custom-call(bf16[2,4,256,128]{3,2,1,0:T(8,128)(2,1)} %clip.1, bf16[3,3,3,128,128]{4,3,2,1,0:T(8,128)(2,1)} %w1.1, bf16[3,3,3,128,128]{4,3,2,1,0:T(8,128)(2,1)} %w2.1, ...), custom_call_target="tpu_custom_call" | custom-call | tf_op jit(solution)/shard_map/pallas_call | solution.py:626
  69.1 2.2 %shard_map.76 = (f32[3456,128]{1,0:T(8,128)}, f32[3456,128]{1,0:T(8,128)}, bf16[2,4,256,128]{3,2,1,0:T(8,128)(2,1)}, bf16[2,4,256,128]{3,2,1,0:T(8,128)(2,1)}) custom-call(bf16[3584,128]{1,0:T(8,128)(2,1)S(1)} %get-tuple-element.12.t1, bf16[3584,128]{1,0:T(8,128)(2,1)S(1)} %get-tuple-element.13.t2, bf16[2,4,256,128]{3,2,1,0:T(8,128)(2,1)S(1)} %get-tuple-element.14.critic, ...), custom_call_target="tpu_custom_call" | custom-call | tf_op jit(solution)/shard_map/pallas_call | solution.py:674

commit v5 on v4

--- a/solution.py
+++ b/solution.py
@@ -422,13 +422,14 @@
             if not last:
                 acc[a] = z
             else:
-                z = (z + acc[a]) * grad_scale
+                z = (z if len(ts) == frames else z + acc[a]) * grad_scale
                 for b in range(3):
                     for q in range(3):
                         at = pl.multiple_of(a * (9 * ch) + (b * 3 + q) * ch, ch)
                         mine[i, pl.ds(at, ch)] = z[b * ch : (b + 1) * ch, q * ch : (q + 1) * ch].astype(BF16)
             return c
-        lax.fori_loop(0, 3, one, 0)
+        for a in range(3):
+            one(a, 0)
 
     for t in range(step):
         loads[2 * t].wait()
@@ -492,17 +493,15 @@
     pass_halo(1, 0)
     turn_input(1, HALO, frames)
     spread_delta(2, 2, 2)
-    weight_grad(1, (2, 3), False, 1)
     wait_halo(1)
     conv_pair(1, w2v, 0, end1)
     for t in (0, 1):
         send_frame(2, t)
         send_rows(2, t)
-    send_out(0, second)
     keep(0)
     turn_input(1, 0, HALO)
     spread_delta(2, 0, 2)
-    weight_grad(1, (0, 1), True, 1)
+    weight_grad(1, local_b, True, 1)
     sum_phase_a(1)
 
     wait_rows(2, local_b)
@@ -511,16 +510,16 @@
         send_frame(3, t)
         send_rows(3, t)
     sum_phase_b(1)
+    send_out(0, second)
     pass_halo(2, 0)
     spread_delta(3, 0, 2)
     weight_grad(0, (0, 1), False, 0)
     pass_halo(2, 1)
-    sum_phase_c(1, order[:2])
     wait_halo(2)
     conv_pair(2, w2t, 2, end2)
     for t in (2, 3):
         send_rows(3, t)
-    sum_phase_c(1, order[2:])
+    sum_phase_c(1, order)
     spread_delta(3, 2, 2)
     weight_grad(0, (2, 3), True, 0)
     sum_phase_a(0)

time: 71.7 us -> 70.7 us (0.986)
  Pallas kernels: 70.7 us -> 69.8 us
    pallas_call x1, Pallas kernels: 68.5 us -> 67.6 us  [on_device(): pl.pallas_call(functools.partial(kernel, n_frame, n_row, grad_scale), out...]
where the time goes in v5:
time: 70.7 us; the launch traced here: 70.6 us
  Pallas kernels  69.8 us (99%)
  between operations  0.8 us (1%)
    pallas_call x1, Pallas kernels, on_device(): pl.pallas_call(functools.partial(kernel, n_frame, n_row, grad_scale), out...  67.6 us
    pallas_call x1, Pallas kernels, on_device(): pl.pallas_call(finish, out_shape=(flat, flat, jax.ShapeDtypeStruct(clip.s...  2.2 us

profile of v5, /device:TPU:0, one launch (start us, length us, event | category | flops | bytes accessed | tf_op | source)
XLA Modules:
  0.0 70.6 jit_solution(11613229007367902727)
XLA Ops:
  0.6 67.6 %shard_map.75 = (bf16[2,4,256,128]{3,2,1,0:T(8,128)(2,1)S(1)}, bf16[2,4,256,128]{3,2,1,0:T(8,128)(2,1)S(1)}, bf16[3584,128]{1,0:T(8,128)(2,1)S(1)}, bf16[3584,128]{1,0:T(8,128)(2,1)S(1)}) custom-call(bf16[2,4,256,128]{3,2,1,0:T(8,128)(2,1)} %clip.1, bf16[3,3,3,128,128]{4,3,2,1,0:T(8,128)(2,1)} %w1.1, bf16[3,3,3,128,128]{4,3,2,1,0:T(8,128)(2,1)} %w2.1, ...), custom_call_target="tpu_custom_call" | custom-call | tf_op jit(solution)/shard_map/pallas_call | solution.py:625
  68.2 2.2 %shard_map.76 = (f32[3456,128]{1,0:T(8,128)}, f32[3456,128]{1,0:T(8,128)}, bf16[2,4,256,128]{3,2,1,0:T(8,128)(2,1)}, bf16[2,4,256,128]{3,2,1,0:T(8,128)(2,1)}) custom-call(bf16[3584,128]{1,0:T(8,128)(2,1)S(1)} %get-tuple-element.12.t1, bf16[3584,128]{1,0:T(8,128)(2,1)S(1)} %get-tuple-element.13.t2, bf16[2,4,256,128]{3,2,1,0:T(8,128)(2,1)S(1)} %get-tuple-element.14.critic, ...), custom_call_target="tpu_custom_call" | custom-call | tf_op jit(solution)/shard_map/pallas_call | solution.py:673

commit v6 on v5

--- a/solution.py
+++ b/solution.py
@@ -132,12 +132,13 @@
         for t in range(step):
             dst[t, :, pl.ds(pl.multiple_of(member * half, half), half)] = src[step * member + t, :, pl.ds(own, half)]
 
-    def frame_copy(k, t):
+    def frame_copy(k, t, part):
         fwd = k < 2
         src, dst = (frames + t, t) if fwd else (t, frames + t)
+        at = (pl.ds(rows - odd * (rows - 1), 1), pl.ds(1 + odd, rows - 1))[part]
         return remote(
-            pads.at[k, src, pl.ds(1, rows)], pads.at[k, dst, pl.ds(1, rows)],
-            f_send.at[k, t], f_recv.at[k, t], {"frame": me_f + 2 if fwd else me_f - 2},
+            pads.at[k, src, at], pads.at[k, dst, at],
+            f_send.at[k, t, part], f_recv.at[k, t, part], {"frame": me_f + 2 if fwd else me_f - 2},
         )
 
     def row_copy(k, f, way):
@@ -181,21 +182,25 @@
             r_send.at[k, f, 0], r_recv.at[k, f, 0], {"row": mate},
         )
 
-    def send_frame(k, t):
+    def send_frames(k, ts):
         there = later if k < 2 else earlier
-
-        @pl.when(there)
-        def _():
-            frame_copy(k, t).start()
-
-        @pl.when(jnp.logical_and(there, facing))
-        def _():
-            corner_copy(k, t).start()
+        for t in ts:
+            @pl.when(there)
+            def _():
+                frame_copy(k, t, 0).start()
+        for t in ts:
+            @pl.when(there)
+            def _():
+                frame_copy(k, t, 1).start()
+
+            @pl.when(jnp.logical_and(there, facing))
+            def _():
+                corner_copy(k, t).start()
 
     def pass_halo(k, t):
         @pl.when(earlier if k < 2 else later)
         def _():
-            frame_copy(k, t).wait_recv()
+            frame_copy(k, t, 0).wait_recv()
             mate_copy(k, t).start()
 
     def wait_halo(k):
@@ -204,6 +209,7 @@
         @pl.when(there)
         def _():
             for t in range(HALO):
+                frame_copy(k, t, 1).wait_recv()
                 mate_copy(k, t).wait_recv()
 
         @pl.when(jnp.logical_and(there, facing))
@@ -441,9 +447,9 @@
     def publish_clip(who, fs):
         @pl.when(who)
         def _():
+            if fs[0] >= frames:
+                send_frames(0, [f - frames for f in fs])
             for f in fs:
-                if f >= frames:
-                    send_frame(0, f - frames)
                 send_rows(0, f)
 
     publish_clip(second, (frames + 1, frames))
@@ -464,8 +470,8 @@
     wait_rows(0, local_f)
     conv_pair(0, w1v, 2, end0)
     for t in (1, 0):
-        send_frame(1, t)
         send_rows(1, frames + t)
+    send_frames(1, (1, 0))
     pass_halo(0, 1)
     pass_halo(0, 0)
     wait_halo(0)
@@ -479,6 +485,7 @@
         cross_copy(1, t).wait_recv()
     wait_rows(1, local_f)
     pass_halo(1, 1)
+    pass_halo(1, 0)
     conv_pair(1, w2v, 2, end1)
     for t in (2, 3):
         send_rows(2, t)
@@ -490,14 +497,13 @@
                 out_copy(i, t).start()
 
     send_out(0, first)
-    pass_halo(1, 0)
     turn_input(1, HALO, frames)
     spread_delta(2, 2, 2)
     wait_halo(1)
     conv_pair(1, w2v, 0, end1)
     for t in (0, 1):
-        send_frame(2, t)
         send_rows(2, t)
+    send_frames(2, (0, 1))
     keep(0)
     turn_input(1, 0, HALO)
     spread_delta(2, 0, 2)
@@ -507,22 +513,23 @@
     wait_rows(2, local_b)
     conv_pair(2, w2t, 0, end2)
     for t in (0, 1):
-        send_frame(3, t)
         send_rows(3, t)
+    send_frames(3, (0, 1))
     sum_phase_b(1)
     send_out(0, second)
     pass_halo(2, 0)
     spread_delta(3, 0, 2)
+    pass_halo(2, 1)
     weight_grad(0, (0, 1), False, 0)
-    pass_halo(2, 1)
     wait_halo(2)
     conv_pair(2, w2t, 2, end2)
     for t in (2, 3):
         send_rows(3, t)
-    sum_phase_c(1, order)
     spread_delta(3, 2, 2)
+    sum_phase_c(1, order[:2])
     weight_grad(0, (2, 3), True, 0)
     sum_phase_a(0)
+    sum_phase_c(1, order[2:])
 
     pass_halo(3, 0)
     pass_halo(3, 1)
@@ -571,7 +578,8 @@
         @pl.when(later if fwd else earlier)
         def _():
             for t in range(HALO):
-                frame_copy(k, t).wait_send()
+                for part in range(2):
+                    frame_copy(k, t, part).wait_send()
 
         @pl.when(jnp.logical_and(later if fwd else earlier, facing))
         def _():
@@ -655,7 +663,7 @@
             sems((3 * step + 2,)),
             sems((2, step)), sems((2, step)),
             sems((2, step)), sems((2, step)),
-            sems((4, HALO)), sems((4, HALO)),
+            sems((4, HALO, 2)), sems((4, HALO, 2)),
             sems((4, HALO)), sems((4, HALO)),
             sems((4, frames + HALO, 2)), sems((4, frames + HALO, 2)),
             sems((2,)), sems((2,)),

time: 70.7 us -> 69.7 us (0.986)
  Pallas kernels: 69.8 us -> 68.8 us
    pallas_call x1, Pallas kernels: 67.6 us -> 66.6 us  [on_device(): pl.pallas_call(functools.partial(kernel, n_frame, n_row, grad_scale), out...]
where the time goes in v6:
time: 69.7 us; the launch traced here: 69.6 us
  Pallas kernels  68.8 us (99%)
  between operations  0.8 us (1%)
    pallas_call x1, Pallas kernels, on_device(): pl.pallas_call(functools.partial(kernel, n_frame, n_row, grad_scale), out...  66.6 us
    pallas_call x1, Pallas kernels, on_device(): pl.pallas_call(finish, out_shape=(flat, flat, jax.ShapeDtypeStruct(clip.s...  2.2 us

profile of v6, /device:TPU:0, one launch (start us, length us, event | category | flops | bytes accessed | tf_op | source)
XLA Modules:
  0.0 69.6 jit_solution(4170814437442560211)
XLA Ops:
  0.6 66.6 %shard_map.75 = (bf16[2,4,256,128]{3,2,1,0:T(8,128)(2,1)S(1)}, bf16[2,4,256,128]{3,2,1,0:T(8,128)(2,1)S(1)}, bf16[3584,128]{1,0:T(8,128)(2,1)S(1)}, bf16[3584,128]{1,0:T(8,128)(2,1)S(1)}) custom-call(bf16[2,4,256,128]{3,2,1,0:T(8,128)(2,1)} %clip.1, bf16[3,3,3,128,128]{4,3,2,1,0:T(8,128)(2,1)} %w1.1, bf16[3,3,3,128,128]{4,3,2,1,0:T(8,128)(2,1)} %w2.1, ...), custom_call_target="tpu_custom_call" | custom-call | tf_op jit(solution)/shard_map/pallas_call | solution.py:633
  67.2 2.2 %shard_map.76 = (f32[3456,128]{1,0:T(8,128)}, f32[3456,128]{1,0:T(8,128)}, bf16[2,4,256,128]{3,2,1,0:T(8,128)(2,1)}, bf16[2,4,256,128]{3,2,1,0:T(8,128)(2,1)}) custom-call(bf16[3584,128]{1,0:T(8,128)(2,1)S(1)} %get-tuple-element.12.t1, bf16[3584,128]{1,0:T(8,128)(2,1)S(1)} %get-tuple-element.13.t2, bf16[2,4,256,128]{3,2,1,0:T(8,128)(2,1)S(1)} %get-tuple-element.14.critic, ...), custom_call_target="tpu_custom_call" | custom-call | tf_op jit(solution)/shard_map/pallas_call | solution.py:681
